TPU v7x, 32 devices: a whole 2x2x4 slice. The times are simulated.
32 devices in a mesh: expert: 2 (over x), dp: 16 (over z, y, core).
Axes of the slice: x: 2, y: 2, z: 4, core: 2. Of those that a mesh axis runs over, the one named last changes fastest.
Arguments:
- grads: bfloat16 [2, 16, 128, 6144], P('expert', 'dp'), may hold values from -16 to 16
- master: float32 [2, 128, 6144], P('expert', 'dp'), may hold values from -0.0625 to 0.0625
- first_moment: float32 [2, 128, 6144], P('expert', 'dp'), may hold values from -0.0029296875 to 0.0029296875
- second_moment: float32 [2, 128, 6144], P('expert', 'dp'), may hold values from 1e-08 to 1e-07
Outputs:
- new_master: float32 [2, 128, 6144], P('expert', 'dp')
- new_first: float32 [2, 128, 6144], P('expert', 'dp')
- new_second: float32 [2, 128, 6144], P('expert', 'dp')
- direction: float32 [2, 128, 6144], P('expert', 'dp')
- new_weights: bfloat16 [2, 128, 6144], P('expert')
All inputs are finite; a program needn't handle non-finite values.
Results may differ from a plain program's by a relative error of at most 0.0004.
Values may be sent and summed in bfloat16 or wider, within the bound.
A program may use at most 64 MiB of HBM per device.

v0:
```python
import jax
import jax.numpy as jnp
from jax import lax
from jax.sharding import PartitionSpec as P

STEP = 10


def shards(grads, master, first_moment, second_moment):
    local = grads[:, 0].astype(jnp.float32)
    summed = lax.psum_scatter(local, "dp", scatter_dimension=1, tiled=True)
    total = lax.psum(jnp.sum(summed * summed), ("expert", "dp"))
    norm = jnp.sqrt(total)
    clip = 1.0 / jnp.maximum(norm, 1.0)
    clipped = clip * summed
    new_first = 0.9 * first_moment + 0.1 * clipped
    new_second = 0.95 * second_moment + 0.05 * (clipped * clipped)
    first_fix = 1.0 - 0.9**STEP
    second_fix = 1.0 - 0.95**STEP
    direction = new_first / first_fix / (jnp.sqrt(new_second / second_fix) + 1e-08)
    new_master = master - 0.001 * (direction + 0.1 * master)
    new_weights = lax.all_gather(new_master.astype(jnp.bfloat16), "dp", axis=1, tiled=True)
    return (new_master, new_first, new_second, direction, new_weights)


def solution(mesh):
    in_specs = (
        P("expert", "dp", None, None),
        P("expert", "dp", None),
        P("expert", "dp", None),
        P("expert", "dp", None),
    )
    out_specs = (
        P("expert", "dp", None),
        P("expert", "dp", None),
        P("expert", "dp", None),
        P("expert", "dp", None),
        P("expert", None, None),
    )
    return jax.shard_map(shards, mesh=mesh, in_specs=in_specs, out_specs=out_specs, check_vma=False)
```

profile of v0, /device:TPU:0, one launch (start us, length us, event | category | flops | bytes accessed | tf_op | source)
XLA Modules:
  0.0 173.7 jit_solution(9061336233872678507)
XLA Ops:
  7.2 0.0 reduce-scatter.2.cloned.1.call-start
  7.2 3.4 %bitcast_convert_fusion = f32[1,128,6144]{2,1,0:T(8,128)} fusion(bf16[1,1,128,6144]{3,2,1,0:T(8,128)(2,1)} %param.4), kind=kLoop, calls=%fused_computation | loop fusion | flops 786432 | bytes 4718592 | tf_op jit(solution)/shard_map/convert_element_type | solution.py:10
  10.6 0.0 copy-start
  10.6 0.0 copy-start.1
  10.6 0.0 copy-start.2
  10.6 0.0 reduce-scatter.2.cloned.1.call-update
  10.6 0.0 all-gather.2.cloned.1.call-start
  10.7 70.1 %reduce-scatter.2.cloned.1.call-done = f32[1,8,6144]{2,1,0:T(8,128)} async-done(((f32[1,128,6144]{2,1,0:T(8,128)}), f32[1,8,6144]{2,1,0:T(8,128)}) %reduce-scatter.2.cloned.1.call-update) | async-done | bytes 196624 | tf_op jit(solution)/shard_map/reduce_scatter | solution.py:11
  80.8 1.6 multiply_reduce_fusion
  82.4 39.9 %psum.7 = f32[]{:T(128)} all-reduce(f32[]{:T(128)} %multiply_reduce_fusion), channel_id=1, replica_groups=mesh['expert'=2,'dp'=16] {'expert','dp'}, use_global_device_ids=true, to_apply=%region_2.0 | all-reduce | flops 1 | bytes 8 | tf_op jit(solution)/shard_map/psum | solution.py:12
  123.0 0.0 copy-done
  123.0 0.0 copy-done.1
  123.0 0.0 copy-done.2
  123.0 1.9 %fusion = (bf16[1,8,6144]{2,1,0:T(8,128)(2,1)}, f32[1,8,6144]{2,1,0:T(8,128)}, f32[1,8,6144]{2,1,0:T(8,128)}, f32[1,8,6144]{2,1,0:T(8,128)}, f32[1,8,6144]{2,1,0:T(8,128)}) fusion(f32[1,8,6144]{2,1,0:T(8,128)S(1)} %copy-done, f32[1,8,6144]{2,1,0:T(8,128)} %reduce-scatter.2.cloned.1.call-done, f32[]{:T(128)S(6)} %div.18, f32[1,8,6144]{2,1,0:T(8,128)S(1)} %copy-done.1, ...), kind=kLoop, calls=%fused_computation.6 | loop fusion | flops 835584 | bytes 1671172 | tf_op jit(solution)/shard_map/convert_element_type | solution.py:22
  125.0 0.0 all-gather.2.cloned.1.call-update
  125.0 39.2 %all-gather.2.cloned.1.call-done = bf16[1,128,6144]{2,1,0:T(8,128)(2,1)} async-done(((bf16[1,8,6144]{2,1,0:T(8,128)(2,1)}), bf16[1,128,6144]{2,1,0:T(8,128)(2,1)}) %all-gather.2.cloned.1.call-update) | async-done | bytes 1572880 | tf_op jit(solution)/shard_map/all_gather | solution.py:22
  164.2 2.7 %copy.10 = bf16[1,128,6144]{2,1,0:T(8,128)(2,1)} copy(bf16[1,128,6144]{2,1,0:T(8,128)(2,1)} %all-gather.2.cloned.1.call-done) | data formatting | bytes 3145728
Async XLA Ops:
  7.2 73.7 %reduce-scatter.2.cloned.1.call-start = ((), (), s32[]{:S(2)}) async-start(), calls=%async_computation.1 | async-start | bytes 3342336 | tf_op jit(solution)/shard_map/reduce_scatter | solution.py:11
  10.6 112.4 %copy-start = (f32[1,8,6144]{2,1,0:T(8,128)S(1)}, f32[1,8,6144]{2,1,0:T(8,128)}, u32[]{:S(2)}) copy-start(f32[1,8,6144]{2,1,0:T(8,128)} %param.5) | copy-start | bytes 589828
  10.6 112.4 %copy-start.1 = (f32[1,8,6144]{2,1,0:T(8,128)S(1)}, f32[1,8,6144]{2,1,0:T(8,128)}, u32[]{:S(2)}) copy-start(f32[1,8,6144]{2,1,0:T(8,128)} %param.6) | copy-start | bytes 589828
  10.6 112.4 %copy-start.2 = (f32[1,8,6144]{2,1,0:T(8,128)S(1)}, f32[1,8,6144]{2,1,0:T(8,128)}, u32[]{:S(2)}) copy-start(f32[1,8,6144]{2,1,0:T(8,128)} %param.7) | copy-start | bytes 589828
  10.6 153.5 %all-gather.2.cloned.1.call-start = ((), (), s32[]{:S(2)}) async-start(), calls=%async_computation.2 | async-start | bytes 1671168 | tf_op jit(solution)/shard_map/all_gather | solution.py:22
Sparse Core Ops, SparseCore 0:
  11.8 68.9 reduce-scatter.1
  125.1 39.0 all-gather.1
where the time goes:
time: 174 us
  waiting for transfers between devices  109 us (63%)
  blocking collectives  39.9 us (23%)
  between operations  14.8 us (9%)
  other arithmetic  6.89 us (4%)
  local copies, waits for them, and re-layouts  2.7 us (2%)
    reduce_scatter x1, waiting for transfers between devices, shards(): summed = lax.psum_scatter(local, 'dp', scatter_dimension=1, tiled=True)  70.1 us
    psum x1, blocking collectives, shards(): total = lax.psum(jnp.sum(summed * summed), ('expert', 'dp'))  39.9 us
    all_gather x1, waiting for transfers between devices, shards(): lax.all_gather(new_master.astype(jnp.bfloat16), 'dp', axis=1, tiled=True)  39.2 us
  transfers between devices with their start and end apart: 2, of which 2 were waited for; matrix products, arithmetic and copies ran while one was open for 0% of the time, Pallas kernels for 0%

commit v1 on v0

v1 whole, which is shorter than its diff:
```python
import functools

import jax
import jax.numpy as jnp
from jax import lax
from jax.experimental import pallas as pl
from jax.experimental.pallas import tpu as pltpu
from jax.sharding import PartitionSpec as P

STEP = 10
MESH = pl.DeviceIdType.MESH


def factors(mesh):
    size = mesh.shape["dp"]
    row = mesh.devices.reshape(-1, size)[0]
    try:
        places = [tuple(d.coords) for d in row]
        cores = size // len(set(places))
        far = len({p[2] for p in places})
    except AttributeError:
        cores, far = 1, size
    return far, size // far // cores, cores


def pieces(width):
    half = width // 2 // 128 * 128
    return [(0, half), (half, width - half)] if half else [(0, width)]


def kernel(sizes, experts, grads, master, first, second, new_master, new_first, new_second, direction, weights,
           raw, own, part, got, master_v, first_v, second_v, norms,
           load_sem, raw_send, raw_recv, part_send, part_recv, norm_send, norm_recv,
           far_send, far_recv, near_send, near_recv, core_send, core_recv):
    A, Y, C = sizes
    B = Y * C
    n = A * B
    width = grads.shape[-1]
    cuts = pieces(width)
    e, me = lax.axis_index("expert"), lax.axis_index("dp")
    a, b = me // B, me % B
    y, c = b // C, b % C

    def turn(value, by, count):
        return (value + by) % count

    def at(za, yb, cc):
        return (e, za * B + yb * C + cc)

    inner = [(dy, dc) for dy in range(Y) for dc in range(C) if dy or dc]
    inner.sort(key=lambda t: -t[0])
    order = sorted(range(1, A), key=lambda k: -min(k, A - k)) + [0]
    everyone = [(de, dd) for de in range(experts) for dd in range(n) if de or dd]

    barrier = pltpu.get_barrier_semaphore()
    for de, dd in everyone:
        pl.semaphore_signal(barrier, inc=1, device_id=(turn(e, de, experts), turn(me, dd, n)), device_id_type=MESH)

    loads = [pltpu.make_async_copy(grads.at[:, b], own, load_sem.at[0])]
    for i, (src, dst) in enumerate(((master, master_v), (first, first_v), (second, second_v))):
        loads.append(pltpu.make_async_copy(src, dst, load_sem.at[i + 1]))
    for copy in loads:
        copy.start()
    pl.semaphore_wait(barrier, len(everyone))

    raws = {}
    for k in order:
        for h, (at0, wide) in enumerate(cuts):
            for i, (dy, dc) in enumerate(inner):
                y2, c2 = turn(y, dy, Y), turn(c, dc, C)
                copy = pltpu.make_async_remote_copy(
                    src_ref=grads.at[turn(a, k, A), y2 * C + c2, :, pl.ds(at0, wide)],
                    dst_ref=raw.at[i, k, :, pl.ds(at0, wide)],
                    send_sem=raw_send.at[i, k, h], recv_sem=raw_recv.at[i, k, h],
                    device_id=at(a, y2, c2), device_id_type=MESH)
                copy.start()
                raws[i, k, h] = copy
    loads[0].wait()

    parts = {}
    for k in order:
        far = turn(a, k, A)
        for h, (at0, wide) in enumerate(cuts):
            cols = pl.ds(at0, wide)
            total = own[far, :, cols].astype(jnp.float32)
            for i in range(len(inner)):
                raws[i, k, h].wait_recv()
                total = total + raw[i, k, :, cols].astype(jnp.float32)
            part[k, :, cols] = total
            if k:
                copy = pltpu.make_async_remote_copy(
                    src_ref=part.at[k, :, cols], dst_ref=got.at[k, :, cols],
                    send_sem=part_send.at[k, h], recv_sem=part_recv.at[k, h],
                    device_id=at(far, y, c), device_id_type=MESH)
                copy.start()
                parts[k, h] = copy

    square = jnp.zeros((1, 128), jnp.float32)
    for h, (at0, wide) in enumerate(cuts):
        cols = pl.ds(at0, wide)
        total = part[0, :, cols]
        for k in order[:-1]:
            parts[k, h].wait_recv()
            total = total + got[k, :, cols]
        part[0, :, cols] = total
        squares = jnp.sum(total * total, axis=0, keepdims=True)
        for j in range(wide // 128):
            square = square + squares[:, j * 128:(j + 1) * 128]
    norms[0] = square
    sent = []
    for i, (de, dd) in enumerate(everyone):
        copy = pltpu.make_async_remote_copy(
            src_ref=norms.at[0], dst_ref=norms.at[i + 1],
            send_sem=norm_send.at[i], recv_sem=norm_recv.at[i],
            device_id=(turn(e, de, experts), turn(me, dd, n)), device_id_type=MESH)
        copy.start()
        sent.append(copy)
    for copy in loads[1:]:
        copy.wait()
    for copy in sent:
        copy.wait_recv()
    whole = jnp.sum(jnp.sum(norms[...], axis=0), axis=1, keepdims=True)
    clip = 1.0 / jnp.maximum(jnp.sqrt(whole), 1.0)

    def forward(where, cols, send, recv, target):
        copy = pltpu.make_async_remote_copy(
            src_ref=weights.at[where[0], where[1], :, cols], dst_ref=weights.at[where[0], where[1], :, cols],
            send_sem=send, recv_sem=recv, device_id=target, device_id_type=MESH)
        copy.start()
        return copy

    fars, nears, partners = {}, {}, {}

    def to_near(k, h, cols):
        for dy in range(1, Y):
            nears[dy, k, h] = forward((turn(a, -k, A), b), cols, near_send.at[dy - 1, k, h], near_recv.at[dy - 1, k, h],
                                      at(a, turn(y, dy, Y), c))

    def to_core(dy, k, h, cols):
        for dc in range(1, C):
            partners[dc, dy, k, h] = forward((turn(a, -k, A), turn(y, -dy, Y) * C + c), cols,
                                             core_send.at[dc - 1, dy, k, h], core_recv.at[dc - 1, dy, k, h],
                                             at(a, y, turn(c, dc, C)))

    first_fix = 1.0 / (1.0 - 0.9**STEP)
    second_fix = 1.0 / (1.0 - 0.95**STEP)
    for h, (at0, wide) in enumerate(cuts):
        cols = pl.ds(at0, wide)
        clipped = clip * part[0, :, cols]
        m = 0.9 * first_v[:, cols] + 0.1 * clipped
        v = 0.95 * second_v[:, cols] + 0.05 * (clipped * clipped)
        d = (m * first_fix) / (jnp.sqrt(v * second_fix) + 1e-08)
        w = master_v[:, cols]
        w = w - 0.001 * (d + 0.1 * w)
        weights[a, b, :, cols] = w.astype(jnp.bfloat16)
        new_master[:, cols] = w
        new_first[:, cols] = m
        new_second[:, cols] = v
        direction[:, cols] = d
        to_near(0, h, cols)
        for k in order[:-1]:
            fars[k, h] = forward((a, b), cols, far_send.at[k, h], far_recv.at[k, h], at(turn(a, k, A), y, c))
        to_core(0, 0, h, cols)
    near_first = sorted(range(1, A), key=lambda k: min(k, A - k))
    for k in near_first:
        for h, (at0, wide) in enumerate(cuts):
            cols = pl.ds(at0, wide)
            fars[k, h].wait_recv()
            to_near(k, h, cols)
            to_core(0, k, h, cols)
    for k in [0] + near_first:
        for h, (at0, wide) in enumerate(cuts):
            cols = pl.ds(at0, wide)
            for dy in range(1, Y):
                nears[dy, k, h].wait_recv()
                to_core(dy, k, h, cols)
    for copy in partners.values():
        copy.wait_recv()
    for copies in (raws, parts, fars, nears, partners):
        for copy in copies.values():
            copy.wait_send()
    for copy in sent:
        copy.wait_send()


def solution(mesh):
    A, Y, C = factors(mesh)
    B = Y * C
    experts = mesh.shape["expert"]
    n = A * B

    def shards(grads, master, first_moment, second_moment):
        rows, width = master.shape[1:]
        H = len(pieces(width))
        state = jax.ShapeDtypeStruct((rows, width), jnp.float32)
        dma = pltpu.SemaphoreType.DMA
        many = experts * n - 1
        vmem = pl.BlockSpec(memory_space=pltpu.VMEM)
        hbm = pl.BlockSpec(memory_space=pl.ANY)
        outs = pl.pallas_call(
            functools.partial(kernel, (A, Y, C), experts),
            out_shape=(state, state, state, state, jax.ShapeDtypeStruct((A, B, rows, width), jnp.bfloat16)),
            in_specs=[hbm] * 4,
            out_specs=(vmem,) * 5,
            scratch_shapes=[
                pltpu.VMEM((max(B - 1, 1), A, rows, width), jnp.bfloat16),
                pltpu.VMEM((A, rows, width), jnp.bfloat16),
                pltpu.VMEM((A, rows, width), jnp.float32),
                pltpu.VMEM((A, rows, width), jnp.float32),
                pltpu.VMEM((rows, width), jnp.float32),
                pltpu.VMEM((rows, width), jnp.float32),
                pltpu.VMEM((rows, width), jnp.float32),
                pltpu.VMEM((many + 1, 1, 128), jnp.float32),
                dma((4,)),
                dma((max(B - 1, 1), A, H)), dma((max(B - 1, 1), A, H)),
                dma((A, H)), dma((A, H)),
                dma((many,)), dma((many,)),
                dma((A, H)), dma((A, H)),
                dma((max(Y - 1, 1), A, H)), dma((max(Y - 1, 1), A, H)),
                dma((max(C - 1, 1), Y, A, H)), dma((max(C - 1, 1), Y, A, H)),
            ],
            compiler_params=pltpu.CompilerParams(collective_id=0, has_side_effects=True),
        )(grads.reshape(A, B, rows, width), master[0], first_moment[0], second_moment[0])
        return tuple(x[None] for x in outs[:4]) + (outs[4].reshape(1, n * rows, width),)

    split = P("expert", "dp", None)
    return jax.shard_map(shards, mesh=mesh, in_specs=(P("expert", "dp", None, None), split, split, split),
                         out_specs=(split, split, split, split, P("expert", None, None)), check_vma=False)
```

time: 174 us -> 60.6 us (0.35)
  waiting for transfers between devices: 109 us -> 0 us
  Pallas kernels: 0 us -> 51.9 us
  blocking collectives: 39.9 us -> 0 us
  between operations: 14.8 us -> 0.65 us
  other arithmetic: 6.89 us -> 0 us
  local copies, waits for them, and re-layouts: 2.7 us -> 7.73 us
    reduce_scatter x1 -> x0, waiting for transfers between devices: 70.1 us -> none  [shards(): summed = lax.psum_scatter(local, 'dp', scatter_dimension=1, tiled=True)]
    pallas_call x0 -> x1, Pallas kernels: none -> 51.9 us  [shards(): pl.pallas_call(functools.partial(kernel, (A, Y, C), experts), out_shape=(...]
    psum x1 -> x0, blocking collectives: 39.9 us -> none  [shards(): total = lax.psum(jnp.sum(summed * summed), ('expert', 'dp'))]
    all_gather x1 -> x0, waiting for transfers between devices: 39.2 us -> none  [shards(): lax.all_gather(new_master.astype(jnp.bfloat16), 'dp', axis=1, tiled=True)]
    convert_element_type x2 -> x0, other arithmetic: 5.31 us -> none  [the longest x1 3.38 us: shards(): local = grads[:, 0].astype(jnp.float32)]
    unnamed x7, local copies, waits for them, and re-layouts: 2.7 us -> 7.73 us
  transfers between devices with their start and end apart: 2 -> 0, of which waited for: 2 -> 0; matrix products, arithmetic and copies ran while one was open for 0% -> 0% of each run, Pallas kernels for 0% -> 0%
where the time goes in v1:
time: 60.6 us; the launch traced here: 60.3 us
  Pallas kernels  51.9 us (86%)
  local copies, waits for them, and re-layouts  7.73 us (13%)
  between operations  0.65 us (1%)
    pallas_call x1, Pallas kernels, shards(): pl.pallas_call(functools.partial(kernel, (A, Y, C), experts), out_shape=(...  51.9 us
    unnamed x7, local copies, waits for them, and re-layouts  7.73 us

profile of v1, /device:TPU:0, one launch (start us, length us, event | category | flops | bytes accessed | tf_op | source)
XLA Modules:
  0.0 60.3 jit_solution(14959913294027634816)
XLA Ops:
  0.6 51.9 %shard_map.83 = (f32[8,6144]{1,0:T(8,128)}, f32[8,6144]{1,0:T(8,128)}, f32[8,6144]{1,0:T(8,128)}, f32[8,6144]{1,0:T(8,128)}, bf16[4,4,8,6144]{3,2,1,0:T(8,128)(2,1)}) custom-call(bf16[4,4,8,6144]{3,2,1,0:T(8,128)(2,1)} %bitcast.10, f32[8,6144]{1,0:T(8,128)} %bitcast.11, f32[8,6144]{1,0:T(8,128)} %bitcast.12, f32[8,6144]{1,0:T(8,128)} %bitcast.13), custom_call_target="tpu_custom_call" | custom-call | tf_op jit(solution)/shard_map/pallas_call | solution.py:200
  52.6 0.0 copy-start
  52.6 1.7 %copy.14 = f32[1,8,6144]{2,1,0:T(8,128)} copy(f32[1,8,6144]{2,1,0:T(8,128)} %bitcast.17) | data formatting | bytes 393216
  54.3 1.6 %copy.15 = f32[1,8,6144]{2,1,0:T(8,128)} copy(f32[1,8,6144]{2,1,0:T(8,128)} %bitcast.16) | data formatting | bytes 393216
  55.9 1.6 %copy.16 = f32[1,8,6144]{2,1,0:T(8,128)} copy(f32[1,8,6144]{2,1,0:T(8,128)} %bitcast.15) | data formatting | bytes 393216
  57.6 1.6 %copy.17 = f32[1,8,6144]{2,1,0:T(8,128)} copy(f32[1,8,6144]{2,1,0:T(8,128)} %bitcast.14) | data formatting | bytes 393216
  59.2 0.0 copy-done
  59.2 1.1 %copy.18 = bf16[1,128,6144]{2,1,0:T(8,128)(2,1)} copy(bf16[1,128,6144]{2,1,0:T(8,128)(2,1)S(1)} %bitcast.9) | data formatting | bytes 3145728
Async XLA Ops:
  52.6 6.6 %copy-start = (bf16[4,4,8,6144]{3,2,1,0:T(8,128)(2,1)S(1)}, bf16[4,4,8,6144]{3,2,1,0:T(8,128)(2,1)}, u32[]{:S(2)}) copy-start(bf16[4,4,8,6144]{3,2,1,0:T(8,128)(2,1)} %get-tuple-element.14) | copy-start | bytes 4718596

commit v2 on v1

--- a/solution.py
+++ b/solution.py
@@ -192,14 +192,13 @@
     def shards(grads, master, first_moment, second_moment):
         rows, width = master.shape[1:]
         H = len(pieces(width))
-        state = jax.ShapeDtypeStruct((rows, width), jnp.float32)
         dma = pltpu.SemaphoreType.DMA
         many = experts * n - 1
         vmem = pl.BlockSpec(memory_space=pltpu.VMEM)
         hbm = pl.BlockSpec(memory_space=pl.ANY)
         outs = pl.pallas_call(
             functools.partial(kernel, (A, Y, C), experts),
-            out_shape=(state, state, state, state, jax.ShapeDtypeStruct((A, B, rows, width), jnp.bfloat16)),
+            out_shape=(pltpu.VMEM((rows, width), jnp.float32),) * 4 + (pltpu.VMEM((A, B, rows, width), jnp.bfloat16),),
             in_specs=[hbm] * 4,
             out_specs=(vmem,) * 5,
             scratch_shapes=[

time: 60.6 us -> 55.2 us (0.911)
  local copies, waits for them, and re-layouts: 7.73 us -> 3.85 us
  Pallas kernels: 51.9 us -> 50.5 us
    unnamed x7 -> x5, local copies, waits for them, and re-layouts: 7.73 us -> 3.85 us
    pallas_call x1, Pallas kernels: 51.9 us -> 50.5 us  [shards(): pl.pallas_call(functools.partial(kernel, (A, Y, C), experts), out_shape=(...]
where the time goes in v2:
time: 55.2 us; the launch traced here: 55 us
  Pallas kernels  50.5 us (91%)
  local copies, waits for them, and re-layouts  3.85 us (7%)
  between operations  0.64 us (1%)
    pallas_call x1, Pallas kernels, shards(): pl.pallas_call(functools.partial(kernel, (A, Y, C), experts), out_shape=(...  50.5 us
    unnamed x5, local copies, waits for them, and re-layouts  3.85 us

profile of v2, /device:TPU:0, one launch (start us, length us, event | category | flops | bytes accessed | tf_op | source)
XLA Modules:
  0.0 55.0 jit_solution(11881895397481458538)
XLA Ops:
  0.6 50.5 %shard_map.83 = (f32[8,6144]{1,0:T(8,128)S(1)}, f32[8,6144]{1,0:T(8,128)S(1)}, f32[8,6144]{1,0:T(8,128)S(1)}, f32[8,6144]{1,0:T(8,128)S(1)}, bf16[4,4,8,6144]{3,2,1,0:T(8,128)(2,1)S(1)}) custom-call(bf16[4,4,8,6144]{3,2,1,0:T(8,128)(2,1)} %bitcast.14, f32[8,6144]{1,0:T(8,128)} %bitcast.15, f32[8,6144]{1,0:T(8,128)} %bitcast.16, f32[8,6144]{1,0:T(8,128)} %bitcast.17), custom_call_target="tpu_custom_call" | custom-call | tf_op jit(solution)/shard_map/pallas_call | solution.py:199
  51.2 0.7 %copy.14 = f32[1,8,6144]{2,1,0:T(8,128)} copy(f32[1,8,6144]{2,1,0:T(8,128)S(1)} %bitcast.13) | data formatting | bytes 393216
  51.8 0.7 %copy.15 = f32[1,8,6144]{2,1,0:T(8,128)} copy(f32[1,8,6144]{2,1,0:T(8,128)S(1)} %bitcast.12) | data formatting | bytes 393216
  52.5 0.7 %copy.16 = f32[1,8,6144]{2,1,0:T(8,128)} copy(f32[1,8,6144]{2,1,0:T(8,128)S(1)} %bitcast.11) | data formatting | bytes 393216
  53.2 0.7 %copy.17 = f32[1,8,6144]{2,1,0:T(8,128)} copy(f32[1,8,6144]{2,1,0:T(8,128)S(1)} %bitcast.10) | data formatting | bytes 393216
  53.9 1.1 %copy.18 = bf16[1,128,6144]{2,1,0:T(8,128)(2,1)} copy(bf16[1,128,6144]{2,1,0:T(8,128)(2,1)S(1)} %bitcast.9) | data formatting | bytes 3145728

commit v3 on v2

v3 whole, which is shorter than its diff:
```python
import functools

import jax
import jax.numpy as jnp
from jax import lax
from jax.experimental import pallas as pl
from jax.experimental.pallas import tpu as pltpu
from jax.sharding import PartitionSpec as P

STEP = 10
CUTS = 3
MESH = pl.DeviceIdType.MESH


def factors(mesh):
    size = mesh.shape["dp"]
    row = mesh.devices.reshape(-1, size)[0]
    try:
        places = [tuple(d.coords) for d in row]
        cores = size // len(set(places))
        far = len({p[2] for p in places})
    except AttributeError:
        cores, far = 1, size
    return far, size // far // cores, cores


def pieces(width):
    tiles = width // 128
    edges = [tiles * i // CUTS * 128 for i in range(CUTS)] + [width]
    return [(p, q - p) for p, q in zip(edges, edges[1:]) if q > p]


def kernel(sizes, experts, grads, master, first, second, new_master, new_first, new_second, direction, weights,
           raw, own, part, arrived, master_v, first_v, second_v, norms,
           load_sem, raw_send, raw_recv, part_send, part_recv, norm_send, norm_recv,
           far_send, far_recv, near_send, near_recv, core_send, core_recv):
    A, Y, C = sizes
    B = Y * C
    n = A * B
    width = grads.shape[-1]
    cuts = pieces(width)
    e, me = lax.axis_index("expert"), lax.axis_index("dp")
    a, b = me // B, me % B
    y, c = b // C, b % C

    def turn(value, by, count):
        return (value + by) % count

    def at(za, yb, cc):
        return (e, za * B + yb * C + cc)

    inner = [(dy, dc) for dy in range(Y) for dc in range(C) if dy or dc]
    inner.sort(key=lambda t: -t[0])
    table = [sorted(range(A), key=lambda t: (-abs(t - z), t)) for z in range(A)]

    def chosen(row):
        pick = row[0]
        for z in range(1, A):
            pick = jnp.where(a == z, row[z], pick)
        return pick

    targets = [chosen([table[z][s] for z in range(A)]) for s in range(A - 1)] + [a]
    everyone = [(de, dd) for de in range(experts) for dd in range(n) if de or dd]

    barrier = pltpu.get_barrier_semaphore()

    def greet(device):
        pl.semaphore_signal(barrier, inc=1, device_id=device, device_id_type=MESH)

    for dy, dc in inner:
        greet(at(a, turn(y, dy, Y), turn(c, dc, C)))
    for de in range(1, experts):
        greet((turn(e, de, experts), me))
    pl.when(a > 0)(lambda: greet(at(a - 1, y, c)))
    pl.when(a < A - 1)(lambda: greet(at(a + 1, y, c)))
    greeted = len(inner) + experts - 1 + jnp.where(a > 0, 1, 0) + jnp.where(a < A - 1, 1, 0)

    loads = [pltpu.make_async_copy(grads.at[:, b], own, load_sem.at[0])]
    for i, (src, dst) in enumerate(((master, master_v), (first, first_v), (second, second_v))):
        loads.append(pltpu.make_async_copy(src, dst, load_sem.at[i + 1]))
    for copy in loads:
        copy.start()
    pl.semaphore_wait(barrier, greeted)

    raws = {}
    for s, t in enumerate(targets):
        for h, (at0, wide) in enumerate(cuts):
            for i, (dy, dc) in enumerate(inner):
                y2, c2 = turn(y, dy, Y), turn(c, dc, C)
                copy = pltpu.make_async_remote_copy(
                    src_ref=grads.at[t, y2 * C + c2, :, pl.ds(at0, wide)],
                    dst_ref=raw.at[i, s, :, pl.ds(at0, wide)],
                    send_sem=raw_send.at[i, s, h], recv_sem=raw_recv.at[i, s, h],
                    device_id=at(a, y2, c2), device_id_type=MESH)
                copy.start()
                raws[i, s, h] = copy
    loads[0].wait()

    def step_on(d, s, t, h):
        cols = pl.ds(*cuts[h])
        ahead = jnp.where(d == 0, jnp.minimum(a + 1, A - 1), jnp.maximum(a - 1, 0))
        return pltpu.make_async_remote_copy(
            src_ref=part.at[s, :, cols], dst_ref=arrived.at[d, t, :, cols],
            send_sem=part_send.at[s, h], recv_sem=part_recv.at[d, t, h],
            device_id=at(ahead, y, c), device_id_type=MESH)

    def add_arrived(d, s, t, h):
        cols = pl.ds(*cuts[h])
        step_on(d, s, t, h).wait_recv()
        part[s, :, cols] = part[s, :, cols] + arrived[d, t, :, cols]

    parts = {}
    square = jnp.zeros((1, 128), jnp.float32)
    for s, t in enumerate(targets):
        for h, (at0, wide) in enumerate(cuts):
            cols = pl.ds(at0, wide)
            total = own[t, :, cols].astype(jnp.float32)
            for i in range(len(inner)):
                raws[i, s, h].wait_recv()
                total = total + raw[i, s, :, cols].astype(jnp.float32)
            part[s, :, cols] = total
            if s < A - 1:
                d = jnp.where(t > a, 0, 1)
                behind = jnp.where(t > a, a, A - 1 - a)
                pl.when(behind > 0)(functools.partial(add_arrived, d, s, t, h))
                parts[s, h] = step_on(d, s, t, h)
                parts[s, h].start()
            else:
                pl.when(a > 0)(functools.partial(add_arrived, 0, s, t, h))
                pl.when(a < A - 1)(functools.partial(add_arrived, 1, s, t, h))
                total = part[s, :, cols]
                squares = jnp.sum(total * total, axis=0, keepdims=True)
                for j in range(wide // 128):
                    square = square + squares[:, j * 128:(j + 1) * 128]
    norms[0] = square
    sent = []
    for i, (de, dd) in enumerate(everyone):
        copy = pltpu.make_async_remote_copy(
            src_ref=norms.at[0], dst_ref=norms.at[i + 1],
            send_sem=norm_send.at[i], recv_sem=norm_recv.at[i],
            device_id=(turn(e, de, experts), turn(me, dd, n)), device_id_type=MESH)
        copy.start()
        sent.append(copy)
    for copy in loads[1:]:
        copy.wait()
    for copy in sent:
        copy.wait_recv()
    whole = jnp.sum(jnp.sum(norms[...], axis=0), axis=1, keepdims=True)
    clip = 1.0 / jnp.maximum(jnp.sqrt(whole), 1.0)

    def forward(where, cols, send, recv, target):
        copy = pltpu.make_async_remote_copy(
            src_ref=weights.at[where[0], where[1], :, cols], dst_ref=weights.at[where[0], where[1], :, cols],
            send_sem=send, recv_sem=recv, device_id=target, device_id_type=MESH)
        return copy

    places = {0: (a, True)}
    for dist in range(1, A):
        places[2 * dist - 1] = (a - dist, a >= dist)
        places[2 * dist] = (a + dist, a + dist < A)

    def near_copy(dy, slot, h):
        where = jnp.clip(places[slot][0], 0, A - 1)
        return forward((where, b), pl.ds(*cuts[h]), near_send.at[dy - 1, slot, h],
                       near_recv.at[dy - 1, slot, h], at(a, turn(y, dy, Y), c))

    def core_copy(dc, dy, slot, h):
        where = jnp.clip(places[slot][0], 0, A - 1)
        return forward((where, turn(y, -dy, Y) * C + c), pl.ds(*cuts[h]), core_send.at[dc - 1, dy, slot, h],
                       core_recv.at[dc - 1, dy, slot, h], at(a, y, turn(c, dc, C)))

    def to_near(slot, h):
        for dy in range(1, Y):
            near_copy(dy, slot, h).start()

    def to_core(dy, slot, h):
        for dc in range(1, C):
            core_copy(dc, dy, slot, h).start()

    def along(slot, up, hop, h):
        dist = (slot + 1) // 2 + hop
        where = jnp.clip(places[slot][0], 0, A - 1)
        there = jnp.minimum(a + hop, A - 1) if up else jnp.maximum(a - hop, 0)
        return pltpu.make_async_remote_copy(
            src_ref=weights.at[where, b, :, pl.ds(*cuts[h])], dst_ref=weights.at[where, b, :, pl.ds(*cuts[h])],
            send_sem=far_send.at[0 if up else 1, dist, h], recv_sem=far_recv.at[0 if up else 1, dist, h],
            device_id=at(there, y, c), device_id_type=MESH)

    def relay(slot, up, h, act="start"):
        dist = (slot + 1) // 2
        if dist % 2:
            return
        for hop in (2, 1):
            if dist + hop < A:
                here = (a + hop < A) if up else (a - hop >= 0)
                pl.when(here)(lambda hop=hop: getattr(along(slot, up, hop, h), act)())

    first_fix = 1.0 / (1.0 - 0.9**STEP)
    second_fix = 1.0 / (1.0 - 0.95**STEP)
    for h, (at0, wide) in enumerate(cuts):
        cols = pl.ds(at0, wide)
        clipped = clip * part[A - 1, :, cols]
        m = 0.9 * first_v[:, cols] + 0.1 * clipped
        v = 0.95 * second_v[:, cols] + 0.05 * (clipped * clipped)
        d = (m * first_fix) / (jnp.sqrt(v * second_fix) + 1e-08)
        w = master_v[:, cols]
        w = w - 0.001 * (d + 0.1 * w)
        weights[a, b, :, cols] = w.astype(jnp.bfloat16)
        new_master[:, cols] = w
        new_first[:, cols] = m
        new_second[:, cols] = v
        direction[:, cols] = d
        to_near(0, h)
        relay(0, True, h)
        relay(0, False, h)
        to_core(0, 0, h)

    def got_far(slot, h):
        dist = (slot + 1) // 2
        up = slot % 2 == 1
        hop = 1 if dist % 2 else 2
        where = jnp.clip(places[slot][0], 0, A - 1)
        block = weights.at[where, b, :, pl.ds(*cuts[h])]
        pltpu.make_async_remote_copy(
            src_ref=block, dst_ref=block, send_sem=far_send.at[0 if up else 1, dist, h],
            recv_sem=far_recv.at[0 if up else 1, dist, h],
            device_id=at(jnp.maximum(a - hop, 0) if up else jnp.minimum(a + hop, A - 1), y, c),
            device_id_type=MESH).wait_recv()
        to_near(slot, h)
        relay(slot, up, h)
        to_core(0, slot, h)

    def got_near(slot, h):
        for dy in range(1, Y):
            near_copy(dy, slot, h).wait_recv()
            to_core(dy, slot, h)

    def got_core(slot, h):
        for dc in range(1, C):
            for dy in range(Y):
                core_copy(dc, dy, slot, h).wait()
        for dy in range(1, Y):
            near_copy(dy, slot, h).wait_send()
        if slot == 0 or slot % 2:
            relay(slot, True, h, "wait_send")
        if slot % 2 == 0:
            relay(slot, False, h, "wait_send")

    slots = sorted(places, key=lambda k: (k + 1) // 2)
    steps = [(slot, h) for slot in slots for h in range(len(cuts))]
    lag = len(cuts) * 2

    def when(slot, work, h):
        if slot:
            pl.when(places[slot][1])(functools.partial(work, slot, h))
        else:
            work(slot, h)

    for i in range(len(steps) + lag):
        if i < len(steps) and steps[i][0]:
            when(steps[i][0], got_far, steps[i][1])
        if i >= lag:
            when(steps[i - lag][0], got_near, steps[i - lag][1])
    for slot, h in steps:
        when(slot, got_core, h)
    for copies in (raws, parts):
        for copy in copies.values():
            copy.wait_send()
    for copy in sent:
        copy.wait_send()


def solution(mesh):
    A, Y, C = factors(mesh)
    B = Y * C
    experts = mesh.shape["expert"]
    n = A * B

    def shards(grads, master, first_moment, second_moment):
        rows, width = master.shape[1:]
        H = len(pieces(width))
        dma = pltpu.SemaphoreType.DMA
        many = experts * n - 1
        vmem = pl.BlockSpec(memory_space=pltpu.VMEM)
        hbm = pl.BlockSpec(memory_space=pl.ANY)
        outs = pl.pallas_call(
            functools.partial(kernel, (A, Y, C), experts),
            out_shape=(pltpu.VMEM((rows, width), jnp.float32),) * 4 + (pltpu.VMEM((A, B, rows, width), jnp.bfloat16),),
            in_specs=[hbm] * 4,
            out_specs=(vmem,) * 5,
            scratch_shapes=[
                pltpu.VMEM((max(B - 1, 1), A, rows, width), jnp.bfloat16),
                pltpu.VMEM((A, rows, width), jnp.bfloat16),
                pltpu.VMEM((A, rows, width), jnp.float32),
                pltpu.VMEM((2, A, rows, width), jnp.float32),
                pltpu.VMEM((rows, width), jnp.float32),
                pltpu.VMEM((rows, width), jnp.float32),
                pltpu.VMEM((rows, width), jnp.float32),
                pltpu.VMEM((many + 1, 1, 128), jnp.float32),
                dma((4,)),
                dma((max(B - 1, 1), A, H)), dma((max(B - 1, 1), A, H)),
                dma((A, H)), dma((2, A, H)),
                dma((many,)), dma((many,)),
                dma((2, A, H)), dma((2, A, H)),
                dma((max(Y - 1, 1), 2 * A - 1, H)), dma((max(Y - 1, 1), 2 * A - 1, H)),
                dma((max(C - 1, 1), Y, 2 * A - 1, H)), dma((max(C - 1, 1), Y, 2 * A - 1, H)),
            ],
            compiler_params=pltpu.CompilerParams(collective_id=0, has_side_effects=True),
        )(grads.reshape(A, B, rows, width), master[0], first_moment[0], second_moment[0])
        return tuple(x[None] for x in outs[:4]) + (outs[4].reshape(1, n * rows, width),)

    split = P("expert", "dp", None)
    return jax.shard_map(shards, mesh=mesh, in_specs=(P("expert", "dp", None, None), split, split, split),
                         out_specs=(split, split, split, split, P("expert", None, None)), check_vma=False)
```

time: 55.2 us -> 55.9 us (1.013)
  Pallas kernels: 50.5 us -> 51.2 us
    pallas_call x1, Pallas kernels: 50.5 us -> 51.2 us  [shards(): pl.pallas_call(functools.partial(kernel, (A, Y, C), experts), out_shape=(...]
where the time goes in v3:
time: 55.9 us; the launch traced here: 55.7 us
  Pallas kernels  51.2 us (92%)
  local copies, waits for them, and re-layouts  3.85 us (7%)
  between operations  0.64 us (1%)
    pallas_call x1, Pallas kernels, shards(): pl.pallas_call(functools.partial(kernel, (A, Y, C), experts), out_shape=(...  51.2 us
    unnamed x5, local copies, waits for them, and re-layouts  3.85 us

profile of v3, /device:TPU:0, one launch (start us, length us, event | category | flops | bytes accessed | tf_op | source)
XLA Modules:
  0.0 55.7 jit_solution(11898306265019561609)
XLA Ops:
  0.6 51.2 %shard_map.83 = (f32[8,6144]{1,0:T(8,128)S(1)}, f32[8,6144]{1,0:T(8,128)S(1)}, f32[8,6144]{1,0:T(8,128)S(1)}, f32[8,6144]{1,0:T(8,128)S(1)}, bf16[4,4,8,6144]{3,2,1,0:T(8,128)(2,1)S(1)}) custom-call(bf16[4,4,8,6144]{3,2,1,0:T(8,128)(2,1)} %bitcast.14, f32[8,6144]{1,0:T(8,128)} %bitcast.15, f32[8,6144]{1,0:T(8,128)} %bitcast.16, f32[8,6144]{1,0:T(8,128)} %bitcast.17), custom_call_target="tpu_custom_call" | custom-call | tf_op jit(solution)/shard_map/pallas_call | solution.py:286
  51.9 0.7 %copy.14 = f32[1,8,6144]{2,1,0:T(8,128)} copy(f32[1,8,6144]{2,1,0:T(8,128)S(1)} %bitcast.13) | data formatting | bytes 393216
  52.6 0.7 %copy.15 = f32[1,8,6144]{2,1,0:T(8,128)} copy(f32[1,8,6144]{2,1,0:T(8,128)S(1)} %bitcast.12) | data formatting | bytes 393216
  53.2 0.7 %copy.16 = f32[1,8,6144]{2,1,0:T(8,128)} copy(f32[1,8,6144]{2,1,0:T(8,128)S(1)} %bitcast.11) | data formatting | bytes 393216
  53.9 0.7 %copy.17 = f32[1,8,6144]{2,1,0:T(8,128)} copy(f32[1,8,6144]{2,1,0:T(8,128)S(1)} %bitcast.10) | data formatting | bytes 393216
  54.6 1.1 %copy.18 = bf16[1,128,6144]{2,1,0:T(8,128)(2,1)} copy(bf16[1,128,6144]{2,1,0:T(8,128)(2,1)S(1)} %bitcast.9) | data formatting | bytes 3145728

commit v4 on v3

--- a/solution.py
+++ b/solution.py
@@ -8,7 +8,7 @@
 from jax.sharding import PartitionSpec as P
 
 STEP = 10
-CUTS = 3
+CUTS = 2
 MESH = pl.DeviceIdType.MESH
 
 
@@ -177,23 +177,15 @@
         for dc in range(1, C):
             core_copy(dc, dy, slot, h).start()
 
-    def along(slot, up, hop, h):
-        dist = (slot + 1) // 2 + hop
-        where = jnp.clip(places[slot][0], 0, A - 1)
-        there = jnp.minimum(a + hop, A - 1) if up else jnp.maximum(a - hop, 0)
-        return pltpu.make_async_remote_copy(
-            src_ref=weights.at[where, b, :, pl.ds(*cuts[h])], dst_ref=weights.at[where, b, :, pl.ds(*cuts[h])],
-            send_sem=far_send.at[0 if up else 1, dist, h], recv_sem=far_recv.at[0 if up else 1, dist, h],
-            device_id=at(there, y, c), device_id_type=MESH)
-
-    def relay(slot, up, h, act="start"):
-        dist = (slot + 1) // 2
-        if dist % 2:
-            return
-        for hop in (2, 1):
-            if dist + hop < A:
-                here = (a + hop < A) if up else (a - hop >= 0)
-                pl.when(here)(lambda hop=hop: getattr(along(slot, up, hop, h), act)())
+    def along(up, dist, h):
+        there = jnp.minimum(a + dist, A - 1) if up else jnp.maximum(a - dist, 0)
+        return forward((a, b), pl.ds(*cuts[h]), far_send.at[0 if up else 1, dist, h],
+                       far_recv.at[0 if up else 1, dist, h], at(there, y, c))
+
+    def spread(h, act="start"):
+        for dist in range(A - 1, 0, -1):
+            pl.when(a + dist < A)(lambda dist=dist: getattr(along(True, dist, h), act)())
+            pl.when(a >= dist)(lambda dist=dist: getattr(along(False, dist, h), act)())
 
     first_fix = 1.0 / (1.0 - 0.9**STEP)
     second_fix = 1.0 / (1.0 - 0.95**STEP)
@@ -210,24 +202,20 @@
         new_first[:, cols] = m
         new_second[:, cols] = v
         direction[:, cols] = d
+        spread(h)
         to_near(0, h)
-        relay(0, True, h)
-        relay(0, False, h)
         to_core(0, 0, h)
 
     def got_far(slot, h):
         dist = (slot + 1) // 2
         up = slot % 2 == 1
-        hop = 1 if dist % 2 else 2
-        where = jnp.clip(places[slot][0], 0, A - 1)
-        block = weights.at[where, b, :, pl.ds(*cuts[h])]
+        block = weights.at[jnp.clip(places[slot][0], 0, A - 1), b, :, pl.ds(*cuts[h])]
+        there = jnp.maximum(a - dist, 0) if up else jnp.minimum(a + dist, A - 1)
         pltpu.make_async_remote_copy(
             src_ref=block, dst_ref=block, send_sem=far_send.at[0 if up else 1, dist, h],
             recv_sem=far_recv.at[0 if up else 1, dist, h],
-            device_id=at(jnp.maximum(a - hop, 0) if up else jnp.minimum(a + hop, A - 1), y, c),
-            device_id_type=MESH).wait_recv()
+            device_id=at(there, y, c), device_id_type=MESH).wait_recv()
         to_near(slot, h)
-        relay(slot, up, h)
         to_core(0, slot, h)
 
     def got_near(slot, h):
@@ -241,14 +229,12 @@
                 core_copy(dc, dy, slot, h).wait()
         for dy in range(1, Y):
             near_copy(dy, slot, h).wait_send()
-        if slot == 0 or slot % 2:
-            relay(slot, True, h, "wait_send")
-        if slot % 2 == 0:
-            relay(slot, False, h, "wait_send")
+        if slot == 0:
+            spread(h, "wait_send")
 
     slots = sorted(places, key=lambda k: (k + 1) // 2)
-    steps = [(slot, h) for slot in slots for h in range(len(cuts))]
-    lag = len(cuts) * 2
+    steps = [(slot, h) for h in range(len(cuts)) for slot in slots]
+    lag = len(slots)
 
     def when(slot, work, h):
         if slot:
@@ -268,6 +254,15 @@
             copy.wait_send()
     for copy in sent:
         copy.wait_send()
+
+
+def write_out(*refs):
+    count = len(refs) // 2
+    copies = [pltpu.make_async_copy(refs[i], refs[count + i], refs[-1].at[i]) for i in range(count)]
+    for copy in copies:
+        copy.start()
+    for copy in copies:
+        copy.wait()
 
 
 def solution(mesh):
@@ -307,6 +302,13 @@
             ],
             compiler_params=pltpu.CompilerParams(collective_id=0, has_side_effects=True),
         )(grads.reshape(A, B, rows, width), master[0], first_moment[0], second_moment[0])
+        outs = pl.pallas_call(
+            write_out,
+            out_shape=tuple(jax.ShapeDtypeStruct(x.shape, x.dtype) for x in outs),
+            in_specs=[vmem] * 5,
+            out_specs=(hbm,) * 5,
+            scratch_shapes=[dma((5,))],
+        )(*(pltpu.with_memory_space_constraint(x, pltpu.VMEM) for x in outs))
         return tuple(x[None] for x in outs[:4]) + (outs[4].reshape(1, n * rows, width),)
 
     split = P("expert", "dp", None)

time: 55.9 us -> 50.6 us (0.905)
  the two profiles are of different devices: /device:TPU:0 before, /device:TPU:17 now
where the time goes in v4:
time: 50.6 us; the launch traced here: 50.5 us
  Pallas kernels  49.8 us (98%)
  between operations  0.64 us (1%)
    pallas_call x1, Pallas kernels, shards(): pl.pallas_call(functools.partial(kernel, (A, Y, C), experts), out_shape=(...  48.4 us
    pallas_call x1, Pallas kernels, shards(): pl.pallas_call(write_out, out_shape=tuple((jax.ShapeDtypeStruct(x.shape,...  1.45 us

profile of v4, /device:TPU:17, one launch (start us, length us, event | category | flops | bytes accessed | tf_op | source)
XLA Modules:
  0.0 50.5 jit_solution(5798354986165872862)
XLA Ops:
  0.6 48.4 %shard_map.83 = (f32[8,6144]{1,0:T(8,128)S(1)}, f32[8,6144]{1,0:T(8,128)S(1)}, f32[8,6144]{1,0:T(8,128)S(1)}, f32[8,6144]{1,0:T(8,128)S(1)}, bf16[4,4,8,6144]{3,2,1,0:T(8,128)(2,1)S(1)}) custom-call(bf16[4,4,8,6144]{3,2,1,0:T(8,128)(2,1)} %bitcast.9, f32[8,6144]{1,0:T(8,128)} %bitcast.10, f32[8,6144]{1,0:T(8,128)} %bitcast.11, f32[8,6144]{1,0:T(8,128)} %bitcast.12), custom_call_target="tpu_custom_call" | custom-call | tf_op jit(solution)/shard_map/pallas_call | solution.py:281
  49.0 1.4 %shard_map.84 = (f32[8,6144]{1,0:T(8,128)}, f32[8,6144]{1,0:T(8,128)}, f32[8,6144]{1,0:T(8,128)}, f32[8,6144]{1,0:T(8,128)}, bf16[4,4,8,6144]{3,2,1,0:T(8,128)(2,1)}) custom-call(f32[8,6144]{1,0:T(8,128)S(1)} %get-tuple-element.15.refs_0_, f32[8,6144]{1,0:T(8,128)S(1)} %get-tuple-element.16.refs_1_, f32[8,6144]{1,0:T(8,128)S(1)} %get-tuple-element.17.refs_2_, ...), custom_call_target="tpu_custom_call" | custom-call | tf_op jit(solution)/shard_map/pallas_call | solution.py:305

commit v5 on v3

--- a/solution.py
+++ b/solution.py
@@ -8,7 +8,8 @@
 from jax.sharding import PartitionSpec as P
 
 STEP = 10
-CUTS = 3
+CUTS = 2
+GATHER_CUTS = 2
 MESH = pl.DeviceIdType.MESH
 
 
@@ -24,9 +25,9 @@
     return far, size // far // cores, cores
 
 
-def pieces(width):
+def pieces(width, count):
     tiles = width // 128
-    edges = [tiles * i // CUTS * 128 for i in range(CUTS)] + [width]
+    edges = [tiles * i // count * 128 for i in range(count)] + [width]
     return [(p, q - p) for p, q in zip(edges, edges[1:]) if q > p]
 
 
@@ -38,7 +39,7 @@
     B = Y * C
     n = A * B
     width = grads.shape[-1]
-    cuts = pieces(width)
+    cuts, gcuts = pieces(width, CUTS), pieces(width, GATHER_CUTS)
     e, me = lax.axis_index("expert"), lax.axis_index("dp")
     a, b = me // B, me % B
     y, c = b // C, b % C
@@ -161,12 +162,12 @@
 
     def near_copy(dy, slot, h):
         where = jnp.clip(places[slot][0], 0, A - 1)
-        return forward((where, b), pl.ds(*cuts[h]), near_send.at[dy - 1, slot, h],
+        return forward((where, b), pl.ds(*gcuts[h]), near_send.at[dy - 1, slot, h],
                        near_recv.at[dy - 1, slot, h], at(a, turn(y, dy, Y), c))
 
     def core_copy(dc, dy, slot, h):
         where = jnp.clip(places[slot][0], 0, A - 1)
-        return forward((where, turn(y, -dy, Y) * C + c), pl.ds(*cuts[h]), core_send.at[dc - 1, dy, slot, h],
+        return forward((where, turn(y, -dy, Y) * C + c), pl.ds(*gcuts[h]), core_send.at[dc - 1, dy, slot, h],
                        core_recv.at[dc - 1, dy, slot, h], at(a, y, turn(c, dc, C)))
 
     def to_near(slot, h):
@@ -182,15 +183,15 @@
         where = jnp.clip(places[slot][0], 0, A - 1)
         there = jnp.minimum(a + hop, A - 1) if up else jnp.maximum(a - hop, 0)
         return pltpu.make_async_remote_copy(
-            src_ref=weights.at[where, b, :, pl.ds(*cuts[h])], dst_ref=weights.at[where, b, :, pl.ds(*cuts[h])],
+            src_ref=weights.at[where, b, :, pl.ds(*gcuts[h])], dst_ref=weights.at[where, b, :, pl.ds(*gcuts[h])],
             send_sem=far_send.at[0 if up else 1, dist, h], recv_sem=far_recv.at[0 if up else 1, dist, h],
             device_id=at(there, y, c), device_id_type=MESH)
 
-    def relay(slot, up, h, act="start"):
+    def relay(slot, up, h, act="start", hops=(2, 1)):
         dist = (slot + 1) // 2
         if dist % 2:
             return
-        for hop in (2, 1):
+        for hop in hops:
             if dist + hop < A:
                 here = (a + hop < A) if up else (a - hop >= 0)
                 pl.when(here)(lambda hop=hop: getattr(along(slot, up, hop, h), act)())
@@ -210,24 +211,25 @@
         new_first[:, cols] = m
         new_second[:, cols] = v
         direction[:, cols] = d
-        to_near(0, h)
+    for h in range(len(gcuts)):
         relay(0, True, h)
         relay(0, False, h)
+        to_near(0, h)
+    for h in range(len(gcuts)):
         to_core(0, 0, h)
 
     def got_far(slot, h):
         dist = (slot + 1) // 2
         up = slot % 2 == 1
         hop = 1 if dist % 2 else 2
-        where = jnp.clip(places[slot][0], 0, A - 1)
-        block = weights.at[where, b, :, pl.ds(*cuts[h])]
+        block = weights.at[jnp.clip(places[slot][0], 0, A - 1), b, :, pl.ds(*gcuts[h])]
+        there = jnp.maximum(a - hop, 0) if up else jnp.minimum(a + hop, A - 1)
         pltpu.make_async_remote_copy(
             src_ref=block, dst_ref=block, send_sem=far_send.at[0 if up else 1, dist, h],
             recv_sem=far_recv.at[0 if up else 1, dist, h],
-            device_id=at(jnp.maximum(a - hop, 0) if up else jnp.minimum(a + hop, A - 1), y, c),
-            device_id_type=MESH).wait_recv()
+            device_id=at(there, y, c), device_id_type=MESH).wait_recv()
+        relay(slot, up, h)
         to_near(slot, h)
-        relay(slot, up, h)
         to_core(0, slot, h)
 
     def got_near(slot, h):
@@ -247,8 +249,9 @@
             relay(slot, False, h, "wait_send")
 
     slots = sorted(places, key=lambda k: (k + 1) // 2)
-    steps = [(slot, h) for slot in slots for h in range(len(cuts))]
-    lag = len(cuts) * 2
+    ranks = [(slot, h) for h in range(len(gcuts)) for slot in slots]
+    steps = sorted(ranks, key=lambda r: ((r[0] + 1) // 2 > 2, r[1], -((r[0] + 1) // 2) % 3))
+    lag = len(slots)
 
     def when(slot, work, h):
         if slot:
@@ -270,6 +273,15 @@
         copy.wait_send()
 
 
+def write_out(*refs):
+    count = len(refs) // 2
+    copies = [pltpu.make_async_copy(refs[i], refs[count + i], refs[-1].at[i]) for i in range(count)]
+    for copy in copies:
+        copy.start()
+    for copy in copies:
+        copy.wait()
+
+
 def solution(mesh):
     A, Y, C = factors(mesh)
     B = Y * C
@@ -278,7 +290,7 @@
 
     def shards(grads, master, first_moment, second_moment):
         rows, width = master.shape[1:]
-        H = len(pieces(width))
+        H, G = len(pieces(width, CUTS)), len(pieces(width, GATHER_CUTS))
         dma = pltpu.SemaphoreType.DMA
         many = experts * n - 1
         vmem = pl.BlockSpec(memory_space=pltpu.VMEM)
@@ -301,12 +313,19 @@
                 dma((max(B - 1, 1), A, H)), dma((max(B - 1, 1), A, H)),
                 dma((A, H)), dma((2, A, H)),
                 dma((many,)), dma((many,)),
-                dma((2, A, H)), dma((2, A, H)),
-                dma((max(Y - 1, 1), 2 * A - 1, H)), dma((max(Y - 1, 1), 2 * A - 1, H)),
-                dma((max(C - 1, 1), Y, 2 * A - 1, H)), dma((max(C - 1, 1), Y, 2 * A - 1, H)),
+                dma((2, A, G)), dma((2, A, G)),
+                dma((max(Y - 1, 1), 2 * A - 1, G)), dma((max(Y - 1, 1), 2 * A - 1, G)),
+                dma((max(C - 1, 1), Y, 2 * A - 1, G)), dma((max(C - 1, 1), Y, 2 * A - 1, G)),
             ],
             compiler_params=pltpu.CompilerParams(collective_id=0, has_side_effects=True),
         )(grads.reshape(A, B, rows, width), master[0], first_moment[0], second_moment[0])
+        outs = pl.pallas_call(
+            write_out,
+            out_shape=tuple(jax.ShapeDtypeStruct(x.shape, x.dtype) for x in outs),
+            in_specs=[vmem] * 5,
+            out_specs=(hbm,) * 5,
+            scratch_shapes=[dma((5,))],
+        )(*(pltpu.with_memory_space_constraint(x, pltpu.VMEM) for x in outs))
         return tuple(x[None] for x in outs[:4]) + (outs[4].reshape(1, n * rows, width),)
 
     split = P("expert", "dp", None)

time: 55.9 us -> 48.5 us (0.87)
  local copies, waits for them, and re-layouts: 3.85 us -> 0 us
  Pallas kernels: 51.2 us -> 47.7 us
    pallas_call x1, Pallas kernels: 51.2 us -> 46.3 us  [shards(): pl.pallas_call(functools.partial(kernel, (A, Y, C), experts), out_shape=(...]
    unnamed x5 -> x0, local copies, waits for them, and re-layouts: 3.85 us -> none
    pallas_call x0 -> x1, Pallas kernels: none -> 1.45 us  [shards(): pl.pallas_call(write_out, out_shape=tuple((jax.ShapeDtypeStruct(x.shape,...]
where the time goes in v5:
time: 48.5 us; the launch traced here: 48.3 us
  Pallas kernels  47.7 us (98%)
  between operations  0.64 us (1%)
    pallas_call x1, Pallas kernels, shards(): pl.pallas_call(functools.partial(kernel, (A, Y, C), experts), out_shape=(...  46.3 us
    pallas_call x1, Pallas kernels, shards(): pl.pallas_call(write_out, out_shape=tuple((jax.ShapeDtypeStruct(x.shape,...  1.45 us

profile of v5, /device:TPU:0, one launch (start us, length us, event | category | flops | bytes accessed | tf_op | source)
XLA Modules:
  0.0 48.3 jit_solution(2730813382993962179)
XLA Ops:
  0.6 46.3 %shard_map.83 = (f32[8,6144]{1,0:T(8,128)S(1)}, f32[8,6144]{1,0:T(8,128)S(1)}, f32[8,6144]{1,0:T(8,128)S(1)}, f32[8,6144]{1,0:T(8,128)S(1)}, bf16[4,4,8,6144]{3,2,1,0:T(8,128)(2,1)S(1)}) custom-call(bf16[4,4,8,6144]{3,2,1,0:T(8,128)(2,1)} %bitcast.9, f32[8,6144]{1,0:T(8,128)} %bitcast.10, f32[8,6144]{1,0:T(8,128)} %bitcast.11, f32[8,6144]{1,0:T(8,128)} %bitcast.12), custom_call_target="tpu_custom_call" | custom-call | tf_op jit(solution)/shard_map/pallas_call | solution.py:298
  46.9 1.4 %shard_map.84 = (f32[8,6144]{1,0:T(8,128)}, f32[8,6144]{1,0:T(8,128)}, f32[8,6144]{1,0:T(8,128)}, f32[8,6144]{1,0:T(8,128)}, bf16[4,4,8,6144]{3,2,1,0:T(8,128)(2,1)}) custom-call(f32[8,6144]{1,0:T(8,128)S(1)} %get-tuple-element.15.refs_0_, f32[8,6144]{1,0:T(8,128)S(1)} %get-tuple-element.16.refs_1_, f32[8,6144]{1,0:T(8,128)S(1)} %get-tuple-element.17.refs_2_, ...), custom_call_target="tpu_custom_call" | custom-call | tf_op jit(solution)/shard_map/pallas_call | solution.py:322

commit v6 on v5

--- a/solution.py
+++ b/solution.py
@@ -45,7 +45,10 @@
     y, c = b // C, b % C
 
     def turn(value, by, count):
-        return (value + by) % count
+        later = value + by % count
+        return later if by % count == 0 else jnp.where(later >= count, later - count, later)
+
+    ys, cs = [turn(y, dy, Y) for dy in range(Y)], [turn(c, dc, C) for dc in range(C)]
 
     def at(za, yb, cc):
         return (e, za * B + yb * C + cc)
@@ -69,7 +72,7 @@
         pl.semaphore_signal(barrier, inc=1, device_id=device, device_id_type=MESH)
 
     for dy, dc in inner:
-        greet(at(a, turn(y, dy, Y), turn(c, dc, C)))
+        greet(at(a, ys[dy], cs[dc]))
     for de in range(1, experts):
         greet((turn(e, de, experts), me))
     pl.when(a > 0)(lambda: greet(at(a - 1, y, c)))
@@ -87,7 +90,7 @@
     for s, t in enumerate(targets):
         for h, (at0, wide) in enumerate(cuts):
             for i, (dy, dc) in enumerate(inner):
-                y2, c2 = turn(y, dy, Y), turn(c, dc, C)
+                y2, c2 = ys[dy], cs[dc]
                 copy = pltpu.make_async_remote_copy(
                     src_ref=grads.at[t, y2 * C + c2, :, pl.ds(at0, wide)],
                     dst_ref=raw.at[i, s, :, pl.ds(at0, wide)],
@@ -157,18 +160,18 @@
 
     places = {0: (a, True)}
     for dist in range(1, A):
-        places[2 * dist - 1] = (a - dist, a >= dist)
-        places[2 * dist] = (a + dist, a + dist < A)
+        places[2 * dist - 1] = (jnp.maximum(a - dist, 0), a >= dist)
+        places[2 * dist] = (jnp.minimum(a + dist, A - 1), a + dist < A)
 
     def near_copy(dy, slot, h):
-        where = jnp.clip(places[slot][0], 0, A - 1)
+        where = places[slot][0]
         return forward((where, b), pl.ds(*gcuts[h]), near_send.at[dy - 1, slot, h],
-                       near_recv.at[dy - 1, slot, h], at(a, turn(y, dy, Y), c))
+                       near_recv.at[dy - 1, slot, h], at(a, ys[dy], c))
 
     def core_copy(dc, dy, slot, h):
-        where = jnp.clip(places[slot][0], 0, A - 1)
-        return forward((where, turn(y, -dy, Y) * C + c), pl.ds(*gcuts[h]), core_send.at[dc - 1, dy, slot, h],
-                       core_recv.at[dc - 1, dy, slot, h], at(a, y, turn(c, dc, C)))
+        where = places[slot][0]
+        return forward((where, ys[-dy % Y] * C + c), pl.ds(*gcuts[h]), core_send.at[dc - 1, dy, slot, h],
+                       core_recv.at[dc - 1, dy, slot, h], at(a, y, cs[dc]))
 
     def to_near(slot, h):
         for dy in range(1, Y):
@@ -180,7 +183,7 @@
 
     def along(slot, up, hop, h):
         dist = (slot + 1) // 2 + hop
-        where = jnp.clip(places[slot][0], 0, A - 1)
+        where = places[slot][0]
         there = jnp.minimum(a + hop, A - 1) if up else jnp.maximum(a - hop, 0)
         return pltpu.make_async_remote_copy(
             src_ref=weights.at[where, b, :, pl.ds(*gcuts[h])], dst_ref=weights.at[where, b, :, pl.ds(*gcuts[h])],
@@ -198,7 +201,7 @@
 
     first_fix = 1.0 / (1.0 - 0.9**STEP)
     second_fix = 1.0 / (1.0 - 0.95**STEP)
-    for h, (at0, wide) in enumerate(cuts):
+    for h, (at0, wide) in enumerate(gcuts):
         cols = pl.ds(at0, wide)
         clipped = clip * part[A - 1, :, cols]
         m = 0.9 * first_v[:, cols] + 0.1 * clipped
@@ -211,7 +214,6 @@
         new_first[:, cols] = m
         new_second[:, cols] = v
         direction[:, cols] = d
-    for h in range(len(gcuts)):
         relay(0, True, h)
         relay(0, False, h)
         to_near(0, h)
@@ -222,7 +224,7 @@
         dist = (slot + 1) // 2
         up = slot % 2 == 1
         hop = 1 if dist % 2 else 2
-        block = weights.at[jnp.clip(places[slot][0], 0, A - 1), b, :, pl.ds(*gcuts[h])]
+        block = weights.at[places[slot][0], b, :, pl.ds(*gcuts[h])]
         there = jnp.maximum(a - hop, 0) if up else jnp.minimum(a + hop, A - 1)
         pltpu.make_async_remote_copy(
             src_ref=block, dst_ref=block, send_sem=far_send.at[0 if up else 1, dist, h],
@@ -251,7 +253,7 @@
     slots = sorted(places, key=lambda k: (k + 1) // 2)
     ranks = [(slot, h) for h in range(len(gcuts)) for slot in slots]
     steps = sorted(ranks, key=lambda r: ((r[0] + 1) // 2 > 2, r[1], -((r[0] + 1) // 2) % 3))
-    lag = len(slots)
+    lag = len(steps)
 
     def when(slot, work, h):
         if slot:

time: 48.5 us -> 48.4 us (level)
  no operation moved by 1% of the time
where the time goes in v6:
time: 48.4 us; the launch traced here: 48.2 us
  Pallas kernels  47.6 us (98%)
  between operations  0.64 us (1%)
    pallas_call x1, Pallas kernels, shards(): pl.pallas_call(functools.partial(kernel, (A, Y, C), experts), out_shape=(...  46.1 us
    pallas_call x1, Pallas kernels, shards(): pl.pallas_call(write_out, out_shape=tuple((jax.ShapeDtypeStruct(x.shape,...  1.45 us

profile of v6, /device:TPU:0, one launch (start us, length us, event | category | flops | bytes accessed | tf_op | source)
XLA Modules:
  0.0 48.2 jit_solution(18336584998631073177)
XLA Ops:
  0.6 46.1 %shard_map.83 = (f32[8,6144]{1,0:T(8,128)S(1)}, f32[8,6144]{1,0:T(8,128)S(1)}, f32[8,6144]{1,0:T(8,128)S(1)}, f32[8,6144]{1,0:T(8,128)S(1)}, bf16[4,4,8,6144]{3,2,1,0:T(8,128)(2,1)S(1)}) custom-call(bf16[4,4,8,6144]{3,2,1,0:T(8,128)(2,1)} %bitcast.9, f32[8,6144]{1,0:T(8,128)} %bitcast.10, f32[8,6144]{1,0:T(8,128)} %bitcast.11, f32[8,6144]{1,0:T(8,128)} %bitcast.12), custom_call_target="tpu_custom_call" | custom-call | tf_op jit(solution)/shard_map/pallas_call | solution.py:300
  46.8 1.4 %shard_map.84 = (f32[8,6144]{1,0:T(8,128)}, f32[8,6144]{1,0:T(8,128)}, f32[8,6144]{1,0:T(8,128)}, f32[8,6144]{1,0:T(8,128)}, bf16[4,4,8,6144]{3,2,1,0:T(8,128)(2,1)}) custom-call(f32[8,6144]{1,0:T(8,128)S(1)} %get-tuple-element.15.refs_0_, f32[8,6144]{1,0:T(8,128)S(1)} %get-tuple-element.16.refs_1_, f32[8,6144]{1,0:T(8,128)S(1)} %get-tuple-element.17.refs_2_, ...), custom_call_target="tpu_custom_call" | custom-call | tf_op jit(solution)/shard_map/pallas_call | solution.py:324
